TPU v7x, 32 devices: a whole 2x2x4 slice. The times are simulated.
32 devices in a mesh: wave: 16 (over z, y, core), lev: 2 (over x).
Axes of the slice: x: 2, y: 2, z: 4, core: 2. Of those that a mesh axis runs over, the one named last changes fastest.
Arguments:
- control: bfloat16 [2, 256, 256, 2, 512], P(None, 'wave', 'lev'), may hold values from -6 to 6
- wave_of_slot: int32 [256], replicated, may hold values from 0 to 255, each once
- legendre: bfloat16 [256, 256, 256], P('wave', 'lev'), may hold values from -0.375 to 0.375
- vertical: bfloat16 [4, 4, 128, 128], replicated, may hold values from -0.5 to 0.5
- points: int32 [256], P('wave'), may hold values from 128 to 512
- lat_band: int32 [256], P('wave'), may hold values from 0 to 7, never falling along the last dimension, each value on 1 to 64 neighbouring positions
- grid_scale: float32 [8, 512], P(None, 'lev'), may hold values from 0.5 to 2
- obs_weight: bfloat16 [256, 512, 512], P('wave', 'lev'), may hold values from 0.19921875 to 1
Outputs:
- increment: bfloat16 [2, 256, 512, 512], P(None, 'wave', 'lev')
- gradient: bfloat16 [2, 256, 256, 2, 512], P(None, 'wave', 'lev')
Inputs may be any that keep to these rules, and one draw needn't show every extreme that they name: `wave_of_slot`: each zonal wavenumber 0 to 255 stands in exactly one slot. `lat_band`: band numbers never fall from one latitude to the next, and each band covers 1 to 64 latitudes.
All inputs are finite; a program needn't handle non-finite values.
Results may differ from a plain program's by a relative error of at most 0.007.
Values may be sent and summed in bfloat16 or wider, within the bound.
A program may use at most 192 MiB of HBM per device.

v0:
```python
import math

import jax
import jax.numpy as jnp
from jax import lax
from jax.sharding import PartitionSpec as P

WAVES = 256
LONGITUDES = 512
LEVELS = 128
VARIABLES = 4
COV_BANDS = 4


def fourier_table(wave_ids, lat_points):
    lon_index = jnp.arange(LONGITUDES, dtype=jnp.int32)
    remainder = wave_ids[None, :, None] * lon_index[None, None, :] % lat_points[:, None, None]
    angles = (
        2.0
        * math.pi
        * remainder.astype(jnp.float32)
        / lat_points.astype(jnp.float32)[:, None, None]
    )
    factor = jnp.where(wave_ids == 0, 1.0, 2.0).astype(jnp.float32) / math.sqrt(4.0 * WAVES)
    inside = lon_index[None, None, :] < lat_points[:, None, None]
    cosine = jnp.where(inside, factor[None, :, None] * jnp.cos(angles), 0.0)
    sine = jnp.where(inside, -factor[None, :, None] * jnp.sin(angles), 0.0)
    return jnp.stack([cosine, sine], axis=2).astype(jnp.bfloat16)


def vertical_apply(field, vertical, live_rows, band_of, forward):
    members, slots, rows_dev = (field.shape[0], field.shape[1], field.shape[2])
    shaped = field.reshape(members, slots, rows_dev, 2, VARIABLES, LEVELS)
    form = "eskpam,alm->eskpal" if forward else "eskpal,alm->eskpam"
    summed = jnp.zeros(shaped.shape, jnp.float32)
    for index_band in range(COV_BANDS):
        partial_value = jnp.einsum(
            form, shaped, vertical[index_band], preferred_element_type=jnp.float32
        )
        chosen = live_rows & (band_of == index_band)
        summed = summed + jnp.where(chosen[None, :, :, None, None, None], partial_value, 0.0)
    return summed.reshape(field.shape).astype(jnp.bfloat16)


def to_bands(values):
    return lax.all_to_all(values, "wave", split_axis=2, concat_axis=1, tiled=True)


def shards(control, wave_of_slot, legendre, vertical, points, lat_band, grid_scale, obs_weight):
    members, slots, rows_dev = (control.shape[0], control.shape[1], control.shape[2])
    slot_start = lax.axis_index("wave") * slots
    row_start = lax.axis_index("lev") * rows_dev
    own_waves = lax.dynamic_slice_in_dim(wave_of_slot, slot_start, slots)
    row_index = row_start + jnp.arange(rows_dev, dtype=jnp.int32)
    totals_n = own_waves[:, None] + row_index[None, :]
    live_rows = totals_n <= WAVES - 1
    band_of = jnp.minimum(totals_n * COV_BANDS // WAVES, COV_BANDS - 1)
    spectral = vertical_apply(control, vertical, live_rows, band_of, True)
    columns = lax.all_to_all(spectral, "lev", split_axis=4, concat_axis=2, tiled=True)
    col_dev = columns.shape[4]
    width = 2 * col_dev
    all_rows = columns.shape[2]
    columns = columns.reshape(members, slots, all_rows, width)
    coeffs = jnp.einsum(
        "skt,eskq->estq",
        lax.all_gather(legendre, "lev", axis=1, tiled=True),
        columns,
        preferred_element_type=jnp.float32,
    )
    coeffs = coeffs.astype(jnp.bfloat16)
    by_lat = to_bands(coeffs)
    wave_count = by_lat.shape[1]
    lat_dev = by_lat.shape[2]
    by_lat = by_lat.reshape(members, wave_count, lat_dev, 2, col_dev)
    fourier = fourier_table(wave_of_slot, points)
    synthesis = jnp.einsum("tspj,estpc->etcj", fourier, by_lat, preferred_element_type=jnp.float32)
    chooser = (
        lat_band[:, None] == jnp.arange(grid_scale.shape[0], dtype=jnp.int32)[None, :]
    ).astype(jnp.float32)
    lat_scale = jnp.dot(chooser, grid_scale, precision=lax.Precision.HIGHEST)
    increment = (synthesis * lat_scale[None, :, :, None]).astype(jnp.bfloat16)
    weighted = (
        increment.astype(jnp.float32) * obs_weight.astype(jnp.float32) * lat_scale[None, :, :, None]
    ).astype(jnp.bfloat16)
    adjoint_fourier = jnp.einsum(
        "tspj,etcj->etspc", fourier, weighted, preferred_element_type=jnp.float32
    )
    adjoint_fourier = adjoint_fourier.astype(jnp.bfloat16).reshape(
        members, lat_dev, wave_count, width
    )
    band_rows = to_bands(adjoint_fourier)
    adjoint_coeffs = jnp.einsum(
        "skt,etsq->eskq",
        lax.all_gather(legendre, "lev", axis=1, tiled=True),
        band_rows,
        preferred_element_type=jnp.float32,
    )
    adjoint_coeffs = adjoint_coeffs.astype(jnp.bfloat16).reshape(
        members, slots, all_rows, 2, col_dev
    )
    rows_back = lax.all_to_all(adjoint_coeffs, "lev", split_axis=2, concat_axis=4, tiled=True)
    gradient = vertical_apply(rows_back, vertical, live_rows, band_of, False)
    return (increment, gradient)


def solution(mesh):
    in_specs = (
        P(None, "wave", "lev", None, None),
        P(),
        P("wave", "lev", None),
        P(),
        P("wave"),
        P("wave"),
        P(None, "lev"),
        P("wave", "lev", None),
    )
    out_specs = (P(None, "wave", "lev", None), P(None, "wave", "lev", None, None))
    return jax.shard_map(shards, mesh=mesh, in_specs=in_specs, out_specs=out_specs, check_vma=False)
```

profile of v0, /device:TPU:29, one launch (start us, length us, event | category | flops | bytes accessed | tf_op | source)
XLA Modules:
  0.0 1020.7 jit_solution(5257670310123423608)
XLA Ops:
  7.2 0.0 copy-start
  7.2 14.1 %reshape.273 = bf16[2,16,128,2,4,128]{5,4,3,2,1,0:T(4,128)(2,1)} reshape(bf16[2,16,128,2,512]{4,3,2,1,0:T(2,128)(2,1)} %param.8) | data formatting | bytes 16777216 | tf_op jit(solution)/shard_map/reshape | solution.py:33
  21.3 11.6 %fusion.28 = f32[4,128,2,16,128,2]{4,1,5,3,2,0:T(8,128)} fusion(bf16[2,16,128,2,4,128]{5,4,3,2,1,0:T(4,128)(2,1)} %reshape.273, bf16[4,4,128,128]{3,2,1,0:T(8,128)(2,1)S(1)} %copy-done.4), kind=kOutput, calls=%fused_computation.35 | convolution fusion | flops 1073741824 | bytes 25296896 | tf_op jit(solution)/shard_map/eskpam,alm->eskpal/dot_general | solution.py:37
  32.9 8.1 fusion.30
  41.0 8.1 fusion.32
  49.1 0.1 dynamic_slice.3
  49.2 0.1 fusion.68
  49.3 0.6 copy-done.5
  49.9 23.9 %fusion.34 = bf16[2,16,128,2,4,128]{2,5,3,1,0,4:T(8,128)(2,1)} fusion(bf16[2,16,128,2,4,128]{5,4,3,2,1,0:T(4,128)(2,1)} %reshape.273, pred[16,128]{1,0:T(8,128)(4,1)S(1)} %get-tuple-element.14, f32[4,128,2,16,128,2]{4,1,5,3,2,0:T(8,128)} %fusion.28, pred[16,128]{1,0:T(8,128)(4,1)S(1)} %get-tuple-element.15, f32[4,128,2,16,128,2]{4,1,5,3,2,0:T(8,128)} %fusion.30, ...), kind=kOutput, calls=%fused_computation.41 | convolution fusion | flops 1107296256 | bytes 67248128 | tf_op jit(solution)/shard_map/eskpam,alm->eskpal/dot_general | solution.py:37
  73.8 10.5 %copy.73 = bf16[2,16,128,2,4,128]{2,5,4,3,1,0:T(8,128)(2,1)} copy(bf16[2,16,128,2,4,128]{2,5,3,1,0,4:T(8,128)(2,1)} %fusion.34) | data formatting | bytes 16777216 | tf_op jit(solution)/shard_map/add | solution.py:41
  84.3 13.1 %copy.74 = bf16[2,16,128,2,512]{2,3,1,0,4:T(2,128)(2,1)} copy(bf16[2,16,128,2,512]{2,4,3,1,0:T(8,128)(2,1)} %bitcast.123) | data formatting | bytes 16777216 | tf_op jit(solution)/shard_map/convert_element_type | solution.py:42
  97.5 6.9 all-to-all-start
  104.4 0.0 all-gather.2.cloned.1.call-start
  104.5 0.7 all-gather.2.cloned.1.call-update
  105.1 113.5 %all-to-all-done = bf16[2,16,128,2,512]{2,3,1,0,4:T(2,128)(2,1)} async-done(((bf16[2,16,128,2,512]{2,3,1,0,4:T(2,128)(2,1)}), bf16[2,16,128,2,512]{2,3,1,0,4:T(2,128)(2,1)}, u32[]{:S(2)}, u32[]{:S(2)}) %all-to-all-start) | async-done | bytes 8388640 | tf_op jit(solution)/shard_map/all_to_all | solution.py:59
  218.6 16.5 %copy.75 = bf16[2,16,128,2,512]{2,4,3,1,0:T(8,128)(2,1)} copy(bf16[2,16,128,2,512]{2,3,1,0,4:T(2,128)(2,1)} %all-to-all-done) | data formatting | bytes 16777216 | tf_op jit(solution)/shard_map/all_to_all | solution.py:59
  235.1 16.8 %copy.76 = bf16[2,16,2,128,2,256]{3,2,5,4,0,1:T(2,128)(2,1)} copy(bf16[2,16,2,128,2,256]{3,5,2,4,1,0:T(8,128)(2,1)} %bitcast.124) | data formatting | bytes 16777216 | tf_op jit(solution)/shard_map/all_to_all | solution.py:59
  251.9 14.0 %reshape.274 = bf16[2,16,256,512]{2,3,0,1:T(8,128)(2,1)} reshape(bf16[2,16,2,128,2,256]{3,2,5,4,0,1:T(2,128)(2,1)} %copy.76) | data formatting | bytes 16777216 | tf_op jit(solution)/shard_map/reshape | solution.py:63
  265.9 9.7 convert_bitcast_fusion
  275.6 21.1 %copy.77 = bf16[2,16,256,512]{3,0,1,2:T(2,128)(2,1)} copy(bf16[2,16,256,512]{2,3,0,1:T(8,128)(2,1)} %convert_bitcast_fusion) | data formatting | bytes 16777216 | tf_op jit(solution)/shard_map/convert_element_type | solution.py:70
  296.7 7.2 all-to-all-start.1
  303.9 6.6 convert_element_type.68
  310.5 0.1 iota_compare_fusion
  310.5 0.2 fusion.73
  310.7 0.1 iota_multiply_fusion
  310.9 121.6 %select_convert_fusion.1 = (bf16[16,256,1,512]{3,1,2,0:T(8,128)(2,1)}, bf16[16,256,1,512]{3,1,2,0:T(8,128)(2,1)}) fusion(f32[256]{0:T(256)S(1)} %get-tuple-element.16, f32[16]{0:T(128)S(1)} %get-tuple-element.19, pred[16]{0:T(512)(128)(4,1)S(1)} %broadcast_compare_fusion, s32[16]{0:T(128)S(1)} %get-tuple-element.18, s32[256,512]{1,0:T(8,128)S(1)} %iota_multiply_fusion, ...), kind=kLoop, calls=%fused_computation.21 | loop fusion | flops 33554432 | bytes 8923280 | tf_op jit(solution)/shard_map/convert.1
  432.5 52.7 %all-to-all-done.1 = bf16[2,16,256,512]{3,0,1,2:T(2,128)(2,1)} async-done(((bf16[2,16,256,512]{3,0,1,2:T(2,128)(2,1)}), bf16[2,16,256,512]{3,0,1,2:T(2,128)(2,1)}, u32[]{:S(2)}, u32[]{:S(2)}) %all-to-all-start.1) | async-done | bytes 8388640 | tf_op jit(solution)/shard_map/all_to_all | solution.py:46
  485.2 11.5 %copy.78 = bf16[2,16,256,512]{3,2,1,0:T(8,128)(2,1)} copy(bf16[2,16,256,512]{3,0,1,2:T(2,128)(2,1)} %all-to-all-done.1) | data formatting | bytes 16777216 | tf_op jit(solution)/shard_map/all_to_all | solution.py:46
  496.7 8.2 copy.79
  504.9 12.5 %reshape.275 = bf16[2,256,16,2,256]{4,3,2,1,0:T(2,128)(2,1)} reshape(bf16[2,16,16,16,512]{4,3,2,1,0:T(8,128)(2,1)} %copy.79) | data formatting | bytes 16777216 | tf_op jit(solution)/shard_map/reshape | solution.py:74
  517.4 17.3 %fusion.40 = bf16[2,16,256,512]{3,2,0,1:T(8,128)(2,1)} fusion(f32[16,256]{1,0:T(8,128)S(1)} %fusion.73, bf16[16,256,1,512]{3,1,2,0:T(8,128)(2,1)} %get-tuple-element.11, bf16[16,256,1,512]{3,1,2,0:T(8,128)(2,1)} %get-tuple-element.10, bf16[2,256,16,2,256]{4,3,2,1,0:T(2,128)(2,1)} %reshape.275), kind=kOutput, calls=%fused_computation.43 | convolution fusion | flops 4307550208 | bytes 25182208 | tf_op jit(solution)/shard_map/tspj,estpc->etcj/dot_general | solution.py:76
  534.7 13.4 %fusion.17 = bf16[16,2,256,256,2]{3,2,4,1,0:T(8,128)(2,1)} fusion(bf16[2,16,256,512]{3,2,0,1:T(8,128)(2,1)} %fusion.40, f32[16,256]{1,0:T(8,128)S(1)} %fusion.73, f32[16,256,512]{2,1,0:T(8,128)} %convert_element_type.68, bf16[16,256,1,512]{3,1,2,0:T(8,128)(2,1)} %get-tuple-element.11, bf16[16,256,1,512]{3,1,2,0:T(8,128)(2,1)} %get-tuple-element.10), kind=kOutput, calls=%fused_computation.26 | convolution fusion | flops 4332716032 | bytes 33570816 | tf_op jit(solution)/shard_map/tspj,etcj->etspc/dot_general | solution.py:85
  548.1 14.6 %copy.81 = bf16[2,16,256,512]{3,1,0,2:T(8,128)(2,1)} copy(bf16[2,16,256,512]{2,3,0,1:T(8,128)(2,1)} %bitcast.129) | data formatting | bytes 16777216 | tf_op jit(solution)/shard_map/reshape | solution.py:88
  562.6 187.8 %all_to_all.63 = bf16[2,16,256,512]{3,1,0,2:T(8,128)(2,1)} all-to-all(bf16[2,16,256,512]{3,1,0,2:T(8,128)(2,1)} %copy.81), channel_id=1, replica_groups=mesh['wave'=16,'lev'=2] {'wave'}, dimensions={2} | all-to-all | bytes 16777216 | tf_op jit(solution)/shard_map/all_to_all | solution.py:46
  750.5 15.5 %copy.83 = bf16[2,16,16,16,512]{4,3,2,1,0:T(8,128)(2,1)} copy(bf16[2,16,16,16,512]{4,2,0,3,1:T(8,128)(2,1)} %bitcast.126) | data formatting | bytes 16777216 | tf_op jit(solution)/shard_map/all_to_all | solution.py:46
  765.9 12.7 %fusion.14 = bf16[16,2,512,256]{3,2,1,0:T(8,128)(2,1)} fusion(bf16[2,256,16,512]{3,2,1,0:T(8,128)(2,1)} %bitcast.121, bf16[16,256,256]{2,1,0:T(8,128)(2,1)S(1)} %copy-done.3), kind=kOutput, calls=%fused_computation.25 | convolution fusion | flops 2151677952 | bytes 18874368 | tf_op jit(solution)/shard_map/skt,etsq->eskq/dot_general | solution.py:92
  778.6 21.1 %copy.85 = bf16[2,16,256,2,256]{4,3,1,0,2:T(2,128)(2,1)} copy(bf16[2,16,256,2,256]{2,4,3,0,1:T(8,128)(2,1)} %bitcast.122) | data formatting | bytes 16777216 | tf_op jit(solution)/shard_map/reshape | solution.py:98
  799.7 7.0 all-to-all-start.3
  806.7 7.7 copy.97
  814.3 84.6 %all-to-all-done.3 = bf16[2,16,256,2,256]{4,3,1,0,2:T(2,128)(2,1)} async-done(((bf16[2,16,256,2,256]{4,3,1,0,2:T(2,128)(2,1)}), bf16[2,16,256,2,256]{4,3,1,0,2:T(2,128)(2,1)}, u32[]{:S(2)}, u32[]{:S(2)}) %all-to-all-start.3) | async-done | bytes 8388640 | tf_op jit(solution)/shard_map/all_to_all | solution.py:101
  899.0 13.6 %copy.86 = bf16[2,16,256,2,256]{4,2,3,1,0:T(8,128)(2,1)} copy(bf16[2,16,256,2,256]{4,3,1,0,2:T(2,128)(2,1)} %all-to-all-done.3) | data formatting | bytes 16777216 | tf_op jit(solution)/shard_map/all_to_all | solution.py:101
  912.6 12.1 %copy.87 = bf16[2,16,128,2,2,256]{2,5,4,3,1,0:T(8,128)(2,1)} copy(bf16[2,16,128,2,2,256]{5,2,4,3,1,0:T(8,128)(2,1)} %bitcast.127) | data formatting | bytes 16777216 | tf_op jit(solution)/shard_map/all_to_all | solution.py:101
  924.7 11.5 %fusion.21 = f32[4,2,16,128,2,128]{3,5,4,2,1,0:T(8,128)} fusion(bf16[2,16,128,2,4,128]{2,5,4,3,1,0:T(8,128)(2,1)} %bitcast.117, bf16[4,4,128,128]{3,2,1,0:T(8,128)(2,1)S(1)} %copy-done.4), kind=kOutput, calls=%fused_computation.28 | convolution fusion | flops 1073741824 | bytes 25296896 | tf_op jit(solution)/shard_map/eskpal,alm->eskpam/dot_general | solution.py:37
  936.2 11.5 %fusion.23 = f32[4,2,16,128,2,128]{3,5,4,2,1,0:T(8,128)} fusion(bf16[2,16,128,2,4,128]{2,5,4,3,1,0:T(8,128)(2,1)} %bitcast.118, bf16[4,4,128,128]{3,2,1,0:T(8,128)(2,1)S(1)} %copy-done.4), kind=kOutput, calls=%fused_computation.30 | convolution fusion | flops 1073741824 | bytes 25296896 | tf_op jit(solution)/shard_map/eskpal,alm->eskpam/dot_general | solution.py:37
  947.7 11.5 %fusion.25 = f32[4,2,16,128,2,128]{3,5,4,2,1,0:T(8,128)} fusion(bf16[2,16,128,2,4,128]{2,5,4,3,1,0:T(8,128)(2,1)} %bitcast.119, bf16[4,4,128,128]{3,2,1,0:T(8,128)(2,1)S(1)} %copy-done.4), kind=kOutput, calls=%fused_computation.32 | convolution fusion | flops 1073741824 | bytes 25296896 | tf_op jit(solution)/shard_map/eskpal,alm->eskpam/dot_general | solution.py:37
  959.2 23.0 %fusion.37 = bf16[2,16,128,2,4,128]{2,5,3,1,0,4:T(8,128)(2,1)} fusion(bf16[2,16,128,2,4,128]{2,5,4,3,1,0:T(8,128)(2,1)} %bitcast.120, pred[16,128]{1,0:T(8,128)(4,1)S(1)} %copy-done.10, f32[4,2,16,128,2,128]{3,5,4,2,1,0:T(8,128)} %fusion.21, pred[16,128]{1,0:T(8,128)(4,1)S(1)} %copy-done.12, f32[4,2,16,128,2,128]{3,5,4,2,1,0:T(8,128)} %fusion.23, ...), kind=kOutput, calls=%fused_computation.42 | convolution fusion | flops 1107296256 | bytes 67248128 | tf_op jit(solution)/shard_map/eskpal,alm->eskpam/dot_general | solution.py:37
  982.1 10.4 %copy.96 = bf16[2,16,128,2,4,128]{2,5,4,3,1,0:T(8,128)(2,1)} copy(bf16[2,16,128,2,4,128]{2,5,3,1,0,4:T(8,128)(2,1)} %fusion.37) | data formatting | bytes 16777216 | tf_op jit(solution)/shard_map/add | solution.py:41
  992.5 21.1 %copy.98 = bf16[2,16,128,2,512]{4,3,2,1,0:T(2,128)(2,1)} copy(bf16[2,16,128,2,512]{2,4,3,1,0:T(8,128)(2,1)} %bitcast.128) | data formatting | bytes 16777216
  (35 shorter events, 0.1 us)
Async XLA Ops:
  7.2 303.4 %copy-start = (f32[8,256]{1,0:T(8,128)S(1)}, f32[8,256]{1,0:T(8,128)}, u32[]{:S(2)}) copy-start(f32[8,256]{1,0:T(8,128)} %param.14) | copy-start | bytes 24580
  7.2 14.1 %copy-start.4 = (bf16[4,4,128,128]{3,2,1,0:T(8,128)(2,1)S(1)}, bf16[4,4,128,128]{3,2,1,0:T(8,128)(2,1)}, u32[]{:S(2)}) copy-start(bf16[4,4,128,128]{3,2,1,0:T(8,128)(2,1)} %param.11) | copy-start | bytes 1572868
  21.3 11.6 %copy-start.2 = (bf16[2,16,128,2,4,128]{5,4,3,2,1,0:T(4,128)(2,1)S(1)}, bf16[2,16,128,2,4,128]{5,4,3,2,1,0:T(4,128)(2,1)}, u32[]{:S(2)}) copy-start(bf16[2,16,128,2,4,128]{5,4,3,2,1,0:T(4,128)(2,1)} %reshape.273) | copy-start | bytes 25165828
  41.0 8.1 copy-start.13
  49.3 0.6 copy-start.5
  49.3 0.6 copy-start.7
  49.3 0.6 copy-start.9
  49.3 0.6 copy-start.11
  97.5 121.2 %all-to-all-start = ((bf16[2,16,128,2,512]{2,3,1,0,4:T(2,128)(2,1)}), bf16[2,16,128,2,512]{2,3,1,0,4:T(2,128)(2,1)}, u32[]{:S(2)}, u32[]{:S(2)}) async-start(bf16[2,16,128,2,512]{2,3,1,0,4:T(2,128)(2,1)} %copy.74), calls=%async_computation | async-start | bytes 16777216 | tf_op jit(solution)/shard_map/all_to_all | solution.py:59
  104.4 161.5 %all-gather.2.cloned.1.call-start = ((), (), s32[]{:S(2)}) async-start(), calls=%async_computation.4 | async-start | bytes 3145728 | tf_op jit(solution)/shard_map/all_gather | solution.py:66
  296.7 188.5 %all-to-all-start.1 = ((bf16[2,16,256,512]{3,0,1,2:T(2,128)(2,1)}), bf16[2,16,256,512]{3,0,1,2:T(2,128)(2,1)}, u32[]{:S(2)}, u32[]{:S(2)}) async-start(bf16[2,16,256,512]{3,0,1,2:T(2,128)(2,1)} %copy.77), calls=%async_computation.1 | async-start | bytes 16777216 | tf_op jit(solution)/shard_map/all_to_all | solution.py:46
  303.8 6.6 copy-start.14
  303.8 6.7 copy-start.15
  750.4 15.5 %copy-start.3 = (bf16[16,256,256]{2,1,0:T(8,128)(2,1)S(1)}, bf16[16,256,256]{2,1,0:T(8,128)(2,1)}, u32[]{:S(2)}) copy-start(bf16[16,256,256]{2,1,0:T(8,128)(2,1)} %all-gather.2.cloned.1.call-done) | copy-start | bytes 6291460
  799.7 99.3 %all-to-all-start.3 = ((bf16[2,16,256,2,256]{4,3,1,0,2:T(2,128)(2,1)}), bf16[2,16,256,2,256]{4,3,1,0,2:T(2,128)(2,1)}, u32[]{:S(2)}, u32[]{:S(2)}) async-start(bf16[2,16,256,2,256]{4,3,1,0,2:T(2,128)(2,1)} %copy.85), calls=%async_computation.3 | async-start | bytes 16777216 | tf_op jit(solution)/shard_map/all_to_all | solution.py:101
  947.6 11.5 %copy-start.6 = (pred[16,128]{1,0:T(8,128)(4,1)S(1)}, pred[16,128]{1,0:T(8,128)(4,1)}, u32[]{:S(2)}) copy-start(pred[16,128]{1,0:T(8,128)(4,1)} %copy-done.5) | copy-start | bytes 6148
  947.6 11.5 %copy-start.8 = (pred[16,128]{1,0:T(8,128)(4,1)S(1)}, pred[16,128]{1,0:T(8,128)(4,1)}, u32[]{:S(2)}) copy-start(pred[16,128]{1,0:T(8,128)(4,1)} %copy-done.7) | copy-start | bytes 6148
  947.7 11.5 %copy-start.10 = (pred[16,128]{1,0:T(8,128)(4,1)S(1)}, pred[16,128]{1,0:T(8,128)(4,1)}, u32[]{:S(2)}) copy-start(pred[16,128]{1,0:T(8,128)(4,1)} %copy-done.9) | copy-start | bytes 6148
  947.7 11.5 %copy-start.12 = (pred[16,128]{1,0:T(8,128)(4,1)S(1)}, pred[16,128]{1,0:T(8,128)(4,1)}, u32[]{:S(2)}) copy-start(pred[16,128]{1,0:T(8,128)(4,1)} %copy-done.11) | copy-start | bytes 6148
  992.5 21.1 %copy-start.1 = (f32[8,256]{1,0:T(8,128)S(1)}, f32[8,256]{1,0:T(8,128)}, u32[]{:S(2)}) copy-start(f32[8,256]{1,0:T(8,128)} %param.14) | copy-start | bytes 24580
Sparse Core Ops, SparseCore 0:
  106.8 57.0 all-gather.1
where the time goes:
time: 1030 us; the launch traced here: 1020 us
  local copies, waits for them, and re-layouts  255 us (25%)
  waiting for transfers between devices  252 us (24%)
  blocking collectives  188 us (18%)
  matrix products  162 us (16%)
  other arithmetic  128 us (12%)
  starting transfers between devices  21.1 us (2%)
  between operations  14.4 us (1%)
    all_to_all x1, blocking collectives, to_bands(): lax.all_to_all(values, 'wave', split_axis=2, concat_axis=1, tiled=True)  188 us
    another operation x1, other arithmetic  122 us
    all_to_all x1, waiting for transfers between devices, shards(): lax.all_to_all(spectral, 'lev', split_axis=4, concat_axis=2, tiled=True)  113 us
    dot_general x8, matrix products, vertical_apply(): jnp.einsum(form, shaped, vertical[index_band], preferred_element_type=jnp...  109 us
    all_to_all x1, waiting for transfers between devices, shards(): lax.all_to_all(adjoint_coeffs, 'lev', split_axis=2, concat_axis=4, tiled=...  84.6 us
    all_to_all x1, waiting for transfers between devices, to_bands(): lax.all_to_all(values, 'wave', split_axis=2, concat_axis=1, tiled=True)  52.7 us
    all_to_all x3, local copies, waits for them, and re-layouts, to_bands(): lax.all_to_all(values, 'wave', split_axis=2, concat_axis=1, tiled=True)  35.2 us
    all_to_all x2, local copies, waits for them, and re-layouts, shards(): lax.all_to_all(spectral, 'lev', split_axis=4, concat_axis=2, tiled=True)  33.2 us
  transfers between devices with their start and end apart: 4, of which 3 were waited for; matrix products, arithmetic and copies ran while one was open for 18% of the time, Pallas kernels for 0%

commit v1 on v0

--- a/solution.py
+++ b/solution.py
@@ -1,8 +1,11 @@
+import functools
 import math
 
 import jax
 import jax.numpy as jnp
 from jax import lax
+from jax.experimental import pallas as pl
+from jax.experimental.pallas import tpu as pltpu
 from jax.sharding import PartitionSpec as P
 
 WAVES = 256
@@ -46,7 +49,7 @@
     return lax.all_to_all(values, "wave", split_axis=2, concat_axis=1, tiled=True)
 
 
-def shards(control, wave_of_slot, legendre, vertical, points, lat_band, grid_scale, obs_weight):
+def shards_plain(control, wave_of_slot, legendre, vertical, points, lat_band, grid_scale, obs_weight):
     members, slots, rows_dev = (control.shape[0], control.shape[1], control.shape[2])
     slot_start = lax.axis_index("wave") * slots
     row_start = lax.axis_index("lev") * rows_dev
@@ -103,6 +106,340 @@
     return (increment, gradient)
 
 
+MESH = pl.DeviceIdType.MESH
+VMEM_BYTES = 64000 * 1024
+
+
+def enter(n_wave, n_lev):
+    me_w, me_l = lax.axis_index("wave"), lax.axis_index("lev")
+    barrier = pltpu.get_barrier_semaphore()
+
+    def greet(d, carry):
+        peer = lax.rem(me_w + d, n_wave)
+        pl.semaphore_signal(barrier, inc=1, device_id=(peer, me_l), device_id_type=MESH)
+        return carry
+
+    lax.fori_loop(1, n_wave, greet, 0)
+    for d in range(1, n_lev):
+        peer = lax.rem(me_l + d, n_lev)
+        pl.semaphore_signal(barrier, inc=1, device_id=(me_w, peer), device_id_type=MESH)
+    pl.semaphore_wait(barrier, n_wave + n_lev - 2)
+    return me_w, me_l
+
+
+def band_masks(wave, row0, rows, waves):
+    total = wave + row0 + lax.broadcasted_iota(jnp.int32, (rows, LEVELS), 0)
+    width = waves // COV_BANDS
+    masks = []
+    for b in range(COV_BANDS):
+        hit = (total >= b * width) & (total < (b + 1) * width)
+        masks.append(jnp.where(hit, 1.0, 0.0).astype(jnp.bfloat16))
+    return masks
+
+
+def banded_dot(x, masks, matrix):
+    stacked = jnp.concatenate([x * mask for mask in masks], axis=1)
+    return jnp.dot(stacked, matrix, preferred_element_type=jnp.float32).astype(jnp.bfloat16)
+
+
+def forward_kernel(n_wave, n_lev, waves, waves_ref, x_ref, lt_ref, v_ref, out_ref,
+                   spec, away, coef, wsend, x_send, x_recv, w_send, w_recv, own_sem):
+    chunks, slots, rows, _ = x_ref.shape
+    lats = lt_ref.shape[1] // n_wave
+    per = v_ref.shape[0] // n_lev
+    me_w, me_l = enter(n_wave, n_lev)
+    row0 = me_l * rows
+
+    def lev_copy(q, d):
+        peer = lax.rem(me_l + d, n_lev)
+        return pltpu.make_async_remote_copy(
+            src_ref=away.at[q, d - 1], dst_ref=spec.at[q, me_l],
+            send_sem=x_send.at[q, d - 1], recv_sem=x_recv.at[q, d - 1],
+            device_id=(me_w, peer), device_id_type=MESH)
+
+    def wave_copy(q, d):
+        peer = lax.rem(me_w + d, n_wave)
+        return pltpu.make_async_remote_copy(
+            src_ref=wsend.at[q, peer], dst_ref=out_ref.at[q, me_w],
+            send_sem=w_send.at[q, d - 1], recv_sem=w_recv.at[q, d - 1],
+            device_id=(peer, me_l), device_id_type=MESH)
+
+    def own_copy(q):
+        return pltpu.make_async_copy(wsend.at[q, me_w], out_ref.at[q, me_w], own_sem.at[q])
+
+    for q in range(chunks):
+        def vertical_slot(s, carry):
+            masks = band_masks(waves_ref[s], row0, rows, waves)
+            for d in list(range(1, n_lev)) + [0]:
+                half = lax.rem(me_l + d, n_lev)
+                for i in range(per):
+                    a = half * per + i
+                    x = x_ref[q, s, :, pl.ds(pl.multiple_of(a * LEVELS, LEVELS), LEVELS)]
+                    y = banded_dot(x, masks, v_ref[a])
+                    if d == 0:
+                        spec[q, me_l, s, :, i * LEVELS:(i + 1) * LEVELS] = y
+                    else:
+                        away[q, d - 1, s, :, i * LEVELS:(i + 1) * LEVELS] = y
+            return carry
+
+        lax.fori_loop(0, slots, vertical_slot, 0)
+        for d in range(1, n_lev):
+            lev_copy(q, d).start()
+
+    for q in range(chunks):
+        for d in range(1, n_lev):
+            lev_copy(q, d).wait_recv()
+
+        def legendre_slot(s, carry):
+            field = jnp.concatenate([spec[q, l, s] for l in range(n_lev)], axis=0)
+            coef[s] = jnp.dot(lt_ref[s], field, preferred_element_type=jnp.float32)
+            return carry
+
+        lax.fori_loop(0, slots, legendre_slot, 0)
+
+        def turn(w, carry):
+            for t in range(lats):
+                wsend[q, w, t] = coef[:, w * lats + t, :].astype(jnp.bfloat16)
+            return carry
+
+        lax.fori_loop(0, n_wave, turn, 0)
+
+        def send(d, carry):
+            wave_copy(q, d).start()
+            return carry
+
+        lax.fori_loop(1, n_wave, send, 0)
+        own_copy(q).start()
+
+    for q in range(chunks):
+        def finish(d, carry):
+            wave_copy(q, d).wait()
+            return carry
+
+        lax.fori_loop(1, n_wave, finish, 0)
+        own_copy(q).wait()
+        for d in range(1, n_lev):
+            lev_copy(q, d).wait_send()
+
+
+def adjoint_kernel(n_wave, n_lev, waves, waves_ref, a_ref, l_ref, v_ref, out_ref,
+                   land, fine, away, back, w_send, w_recv, x_send, x_recv):
+    chunks, _, lats, slots, cols = a_ref.shape
+    rows = out_ref.shape[2]
+    per = v_ref.shape[0] // n_lev
+    me_w, me_l = enter(n_wave, n_lev)
+    row0 = me_l * rows
+
+    def wave_copy(q, d):
+        peer = lax.rem(me_w + d, n_wave)
+        return pltpu.make_async_remote_copy(
+            src_ref=a_ref.at[q, peer], dst_ref=land.at[q, me_w],
+            send_sem=w_send.at[q, d - 1], recv_sem=w_recv.at[q, d - 1],
+            device_id=(peer, me_l), device_id_type=MESH)
+
+    def lev_copy(q, d):
+        peer = lax.rem(me_l + d, n_lev)
+        return pltpu.make_async_remote_copy(
+            src_ref=away.at[q, d - 1], dst_ref=back.at[q, me_l],
+            send_sem=x_send.at[q, d - 1], recv_sem=x_recv.at[q, d - 1],
+            device_id=(me_w, peer), device_id_type=MESH)
+
+    for q in range(chunks):
+        def send(d, carry):
+            wave_copy(q, d).start()
+            return carry
+
+        lax.fori_loop(1, n_wave, send, 0)
+        land[q, me_w] = a_ref[q, me_w]
+
+    for q in range(chunks):
+        def arrive(d, carry):
+            wave_copy(q, d).wait_recv()
+            return carry
+
+        lax.fori_loop(1, n_wave, arrive, 0)
+
+        def widen(w, carry):
+            base = pl.multiple_of(w * lats, lats)
+            fine[pl.ds(base, lats)] = land[q, w].astype(jnp.float32)
+            return carry
+
+        lax.fori_loop(0, n_wave, widen, 0)
+
+        def legendre_slot(s, carry):
+            field = fine[:, s, :].astype(jnp.bfloat16)
+            for d in range(n_lev):
+                half = lax.rem(me_l + d, n_lev)
+                table = l_ref[s, pl.ds(pl.multiple_of(half * rows, rows), rows), :]
+                y = jnp.dot(table, field, preferred_element_type=jnp.float32).astype(jnp.bfloat16)
+                if d == 0:
+                    back[q, me_l, s] = y
+                else:
+                    away[q, d - 1, s] = y
+            return carry
+
+        lax.fori_loop(0, slots, legendre_slot, 0)
+        for d in range(1, n_lev):
+            lev_copy(q, d).start()
+
+    for q in range(chunks):
+        for d in range(1, n_lev):
+            lev_copy(q, d).wait()
+
+        def vertical_slot(s, carry):
+            masks = band_masks(waves_ref[s], row0, rows, waves)
+            for l in range(n_lev):
+                for i in range(per):
+                    a = l * per + i
+                    x = back[q, l, s, :, i * LEVELS:(i + 1) * LEVELS]
+                    out_ref[q, s, :, a * LEVELS:(a + 1) * LEVELS] = banded_dot(x, masks, v_ref[a])
+            return carry
+
+        lax.fori_loop(0, slots, vertical_slot, 0)
+
+    for q in range(chunks):
+        def drain(d, carry):
+            wave_copy(q, d).wait_send()
+            return carry
+
+        lax.fori_loop(1, n_wave, drain, 0)
+
+
+SIN_TERMS = [(-1.0) ** i * (2.0 * math.pi) ** (2 * i + 1) / math.factorial(2 * i + 1) for i in range(10)]
+COS_TERMS = [(-1.0) ** i * (2.0 * math.pi) ** (2 * i) / math.factorial(2 * i) for i in range(10)]
+
+
+def horner(terms, square):
+    value = jnp.full_like(square, terms[-1])
+    for term in terms[-2::-1]:
+        value = value * square + term
+    return value
+
+
+def grid_kernel(waves_ref, points_ref, x_ref, scale_ref, weight_ref, inc_ref, adj_ref, table):
+    members, _, cols, longs = inc_ref.shape
+    waves = waves_ref.shape[0]
+    points = points_ref[pl.program_id(0)]
+    n = points.astype(jnp.float32)
+    piece = 32
+    inverse = 1.0 / jnp.full((1, longs), n, jnp.float32)
+    lane = lax.broadcasted_iota(jnp.int32, (1, longs), 1)
+    inside = jnp.where(lane < points, 1.0, 0.0) / math.sqrt(4.0 * waves)
+
+    def build(i, carry):
+        base = pl.multiple_of(i * piece, piece)
+        wave = waves_ref[pl.ds(base, piece), :]
+        product = wave * lane.astype(jnp.float32)
+        turns = jnp.floor(product * inverse + 0.5)
+        x = (product - turns * n) * inverse
+        square = x * x
+        gain = jnp.where(wave == 0.0, 1.0, 2.0) * inside
+        table[pl.ds(base, piece), :] = (gain * horner(COS_TERMS, square)).astype(jnp.bfloat16)
+        sine = (-gain) * (x * horner(SIN_TERMS, square))
+        table[pl.ds(pl.multiple_of(waves + base, piece), piece), :] = sine.astype(jnp.bfloat16)
+        return carry
+
+    lax.fori_loop(0, waves // piece, build, 0)
+    scale = scale_ref[0]
+    for e in range(members):
+        coeffs = jnp.concatenate([x_ref[2 * e + p, :, 0].reshape(waves, cols) for p in range(2)], axis=0)
+        synthesis = lax.dot_general(coeffs, table[...], (((0,), (0,)), ((), ())),
+                                    preferred_element_type=jnp.float32)
+        increment = (synthesis * scale).astype(jnp.bfloat16)
+        inc_ref[e, 0] = increment
+        weighted = (increment.astype(jnp.float32) * weight_ref[0].astype(jnp.float32) * scale)
+        adjoint = lax.dot_general(table[...], weighted.astype(jnp.bfloat16), (((1,), (1,)), ((), ())),
+                                  preferred_element_type=jnp.float32).astype(jnp.bfloat16)
+        for p in range(2):
+            part = adjoint[p * waves:(p + 1) * waves]
+            adj_ref[2 * e + p, :, 0] = part.reshape(adj_ref.shape[1], adj_ref.shape[3], cols)
+
+
+def shards_kernels(n_wave, n_lev, control, wave_of_slot, legendre, vertical, points, lat_band, grid_scale, obs_weight):
+    members, slots, rows = control.shape[:3]
+    waves = wave_of_slot.shape[0]
+    variables = vertical.shape[1]
+    columns = control.shape[4]
+    cols = columns // n_lev
+    lats, _, longs = obs_weight.shape
+    chunks = 2 * members
+    bf16, f32 = jnp.bfloat16, jnp.float32
+    own_waves = lax.dynamic_slice_in_dim(wave_of_slot, lax.axis_index("wave") * slots, slots)
+    table = lax.all_gather(legendre, "lev", axis=1, tiled=True)
+    x = control.transpose(0, 3, 1, 2, 4).reshape(chunks, slots, rows, columns)
+    stack_f = vertical.transpose(1, 0, 3, 2).reshape(variables, COV_BANDS * LEVELS, LEVELS)
+    stack_g = vertical.transpose(1, 0, 2, 3).reshape(variables, COV_BANDS * LEVELS, LEVELS)
+    vmem = pl.BlockSpec(memory_space=pltpu.VMEM)
+    smem = pl.BlockSpec(memory_space=pltpu.SMEM)
+    dma = pltpu.SemaphoreType.DMA
+    by_lat = pl.pallas_call(
+        functools.partial(forward_kernel, n_wave, n_lev, waves),
+        out_shape=jax.ShapeDtypeStruct((chunks, n_wave, lats, slots, cols), bf16),
+        in_specs=[smem, vmem, vmem, vmem],
+        out_specs=pl.BlockSpec(memory_space=pl.ANY),
+        scratch_shapes=[
+            pltpu.VMEM((chunks, n_lev, slots, rows, cols), bf16),
+            pltpu.VMEM((chunks, n_lev - 1, slots, rows, cols), bf16),
+            pltpu.VMEM((slots, n_wave * lats, cols), f32),
+            pltpu.VMEM((chunks, n_wave, lats, slots, cols), bf16),
+            dma((chunks, n_lev - 1)), dma((chunks, n_lev - 1)),
+            dma((chunks, n_wave - 1)), dma((chunks, n_wave - 1)), dma((chunks,)),
+        ],
+        compiler_params=pltpu.CompilerParams(collective_id=0, has_side_effects=True, vmem_limit_bytes=VMEM_BYTES),
+        name="forward",
+    )(own_waves, x, table.transpose(0, 2, 1), stack_f)
+    chooser = (
+        lat_band[:, None] == jnp.arange(grid_scale.shape[0], dtype=jnp.int32)[None, :]
+    ).astype(f32)
+    lat_scale = jnp.dot(chooser, grid_scale, precision=lax.Precision.HIGHEST)
+    field_spec = pl.BlockSpec((chunks, n_wave, 1, slots, cols), lambda t: (0, 0, t, 0, 0))
+    increment, adjoint = pl.pallas_call(
+        grid_kernel,
+        grid=(lats,),
+        out_shape=[
+            jax.ShapeDtypeStruct((members, lats, cols, longs), bf16),
+            jax.ShapeDtypeStruct((chunks, n_wave, lats, slots, cols), bf16),
+        ],
+        in_specs=[
+            pl.BlockSpec((waves, 1), lambda t: (0, 0)),
+            smem,
+            field_spec,
+            pl.BlockSpec((1, cols, 1), lambda t: (t, 0, 0)),
+            pl.BlockSpec((1, cols, longs), lambda t: (t, 0, 0)),
+        ],
+        out_specs=[pl.BlockSpec((members, 1, cols, longs), lambda t: (0, t, 0, 0)), field_spec],
+        scratch_shapes=[pltpu.VMEM((2 * waves, longs), bf16)],
+        compiler_params=pltpu.CompilerParams(vmem_limit_bytes=VMEM_BYTES // 2),
+        name="grid",
+    )(wave_of_slot.astype(f32)[:, None], points, by_lat, lat_scale[:, :, None], obs_weight)
+    gradient = pl.pallas_call(
+        functools.partial(adjoint_kernel, n_wave, n_lev, waves),
+        out_shape=jax.ShapeDtypeStruct((chunks, slots, rows, columns), bf16),
+        in_specs=[smem, vmem, vmem, vmem],
+        out_specs=vmem,
+        scratch_shapes=[
+            pltpu.VMEM((chunks, n_wave, lats, slots, cols), bf16),
+            pltpu.VMEM((n_wave * lats, slots, cols), f32),
+            pltpu.VMEM((chunks, n_lev - 1, slots, rows, cols), bf16),
+            pltpu.VMEM((chunks, n_lev, slots, rows, cols), bf16),
+            dma((chunks, n_wave - 1)), dma((chunks, n_wave - 1)),
+            dma((chunks, n_lev - 1)), dma((chunks, n_lev - 1)),
+        ],
+        compiler_params=pltpu.CompilerParams(collective_id=1, has_side_effects=True, vmem_limit_bytes=VMEM_BYTES),
+        name="adjoint",
+    )(own_waves, adjoint, table, stack_g)
+    gradient = gradient.reshape(members, 2, slots, rows, columns).transpose(0, 2, 3, 1, 4)
+    return (increment, gradient)
+
+
+def shards(n_wave, n_lev, *arrays):
+    slots, rows, columns = arrays[0].shape[1], arrays[0].shape[2], arrays[0].shape[4]
+    whole_tiles = slots % 16 == 0 and rows % 128 == 0 and columns % (n_lev * LEVELS) == 0
+    if whole_tiles and n_lev > 1:
+        return shards_kernels(n_wave, n_lev, *arrays)
+    return shards_plain(*arrays)
+
+
 def solution(mesh):
     in_specs = (
         P(None, "wave", "lev", None, None),
@@ -115,4 +452,5 @@
         P("wave", "lev", None),
     )
     out_specs = (P(None, "wave", "lev", None), P(None, "wave", "lev", None, None))
-    return jax.shard_map(shards, mesh=mesh, in_specs=in_specs, out_specs=out_specs, check_vma=False)
+    body = functools.partial(shards, mesh.shape["wave"], mesh.shape["lev"])
+    return jax.shard_map(body, mesh=mesh, in_specs=in_specs, out_specs=out_specs, check_vma=False)

time: 1030 us -> 581 us (0.56)
  Pallas kernels: 0 us -> 499 us
  waiting for transfers between devices: 252 us -> 21.1 us
  local copies, waits for them, and re-layouts: 255 us -> 45.1 us
  blocking collectives: 188 us -> 0 us
  matrix products: 162 us -> 0.19 us
  other arithmetic: 128 us -> 0.68 us
  starting transfers between devices: 21.1 us -> 0.04 us
    pallas_call x0 -> x3, Pallas kernels: none -> 499 us  [the longest x1 228 us: shards_kernels(): pl.pallas_call(functools.partial(adjoint_kernel, n_wave, n_lev, waves), o...]
    all_to_all x3 -> x0, waiting for transfers between devices: 251 us -> none  [the longest x1 113 us: shards(): lax.all_to_all(spectral, 'lev', split_axis=4, concat_axis=2, tiled=True)]
    all_to_all x1 -> x0, blocking collectives: 188 us -> none  [to_bands(): lax.all_to_all(values, 'wave', split_axis=2, concat_axis=1, tiled=True)]
    dot_general x13 -> x1, matrix products: 162 us -> 0.19 us  [shards_kernels(): lat_scale = jnp.dot(chooser, grid_scale, precision=lax.Precision.HIGHEST)]
    another operation x1 -> x0, other arithmetic: 122 us -> none
    all_to_all x7 -> x0, local copies, waits for them, and re-layouts: 94.1 us -> none  [the longest x3 35.2 us: to_bands(): lax.all_to_all(values, 'wave', split_axis=2, concat_axis=1, tiled=True)]
    reshape x5 -> x1, local copies, waits for them, and re-layouts: 76.2 us -> 16.4 us  [shards_kernels(): gradient.reshape(members, 2, slots, rows, columns).transpose(0, 2, 3, 1, 4)]
    convert_element_type x2 -> x0, local copies, waits for them, and re-layouts: 34.2 us -> none  [the longest x1 21.1 us: shards(): coeffs = coeffs.astype(jnp.bfloat16)]
  transfers between devices with their start and end apart: 4 -> 1, of which waited for: 3 -> 1; matrix products, arithmetic and copies ran while one was open for 18% -> 3% of each run, Pallas kernels for 0% -> 0%
where the time goes in v1:
time: 581 us; the launch traced here: 580 us
  Pallas kernels  499 us (86%)
  local copies, waits for them, and re-layouts  45.1 us (8%)
  waiting for transfers between devices  21.1 us (4%)
  between operations  14.1 us (2%)
    pallas_call x1, Pallas kernels, shards_kernels(): pl.pallas_call(functools.partial(adjoint_kernel, n_wave, n_lev, waves), o...  228 us
    pallas_call x1, Pallas kernels, shards_kernels(): pl.pallas_call(functools.partial(forward_kernel, n_wave, n_lev, waves), o...  226 us
    pallas_call x1, Pallas kernels, shards_kernels(): pl.pallas_call(grid_kernel, grid=(lats,), out_shape=[jax.ShapeDtypeStruct...  44.9 us
    all_gather x1, waiting for transfers between devices, shards_kernels(): table = lax.all_gather(legendre, 'lev', axis=1, tiled=True)  20.4 us
    reshape x1, local copies, waits for them, and re-layouts, shards_kernels(): gradient.reshape(members, 2, slots, rows, columns).transpose(0, 2, 3, 1, 4)  16.4 us
  transfers between devices with their start and end apart: 1, of which 1 were waited for; matrix products, arithmetic and copies ran while one was open for 3% of the time, Pallas kernels for 0%

profile of v1, /device:TPU:29, one launch (start us, length us, event | category | flops | bytes accessed | tf_op | source)
XLA Modules:
  0.0 580.4 jit_solution(16769338127421839574)
XLA Ops:
  7.2 0.0 copy-start
  7.2 0.0 all-gather.2.cloned.1.call-start
  7.2 0.7 all-gather.2.cloned.1.call-update
  7.9 0.7 convert_element_type.4
  8.6 1.3 dynamic_slice.3.waves_ref
  9.9 0.0 copy-start.7
  10.0 0.0 copy-start.8
  10.0 8.8 %copy.15 = bf16[2,2,16,128,512]{4,3,2,1,0:T(8,128)(2,1)} copy(bf16[2,2,16,128,512]{4,1,3,2,0:T(2,128)(2,1)} %bitcast.17) | data formatting | bytes 16777216 | tf_op jit(solution)/shard_map/transpose | solution.py:369
  18.8 0.0 copy-done.7
  18.8 1.1 copy.16
  19.9 0.0 copy-done
  19.9 0.0 copy-done.8
  19.9 0.2 convolution_bitcast_fusion
  20.0 2.0 copy.19.scale_ref
  22.0 0.1 copy.18.waves_ref
  22.2 0.9 copy.20
  23.0 20.4 %all-gather.2.cloned.1.call-done.l_ref = bf16[16,256,256]{2,1,0:T(8,128)(2,1)} async-done(((bf16[16,128,256]{2,1,0:T(8,128)(2,1)}), bf16[16,256,256]{2,1,0:T(8,128)(2,1)}) %all-gather.2.cloned.1.call-update) | async-done | bytes 2097168 | tf_op jit(solution)/shard_map/all_gather | solution.py:368
  43.4 3.9 copy.17.lt_ref
  47.3 0.0 copy-start.6
  47.3 226.1 %forward.1.x_ref = bf16[4,16,16,16,256]{4,3,2,1,0:T(8,128)(2,1)} custom-call(s32[16]{0:T(128)} %dynamic_slice.3.waves_ref, bf16[4,16,128,512]{3,2,1,0:T(8,128)(2,1)} %bitcast.15, bf16[16,256,256]{2,1,0:T(8,128)(2,1)} %copy.17.lt_ref, bf16[4,512,128]{2,1,0:T(8,128)(2,1)} %bitcast.21), custom_call_target="tpu_custom_call" | custom-call | tf_op jit(solution)/shard_map/forward/pallas_call | solution.py:375
  273.4 0.0 copy-done.6
  273.5 0.0 copy-start.2
  273.5 3.4 copy-done.2
  276.8 0.0 copy-start.4
  276.8 1.6 copy-done.4
  278.4 0.0 copy-start.5
  278.4 2.2 copy-done.5
  280.6 44.9 %grid.1 = (bf16[2,16,256,512]{3,2,1,0:T(8,128)(2,1)}, bf16[4,16,16,16,256]{4,3,2,1,0:T(8,128)(2,1)S(1)}) custom-call(f32[256,1]{1,0:T(8,128)S(1)} %copy.18.waves_ref, s32[16]{0:T(128)S(1)} %copy-done.6, bf16[4,16,16,16,256]{4,3,2,1,0:T(8,128)(2,1)S(1)} %copy-done.2, f32[16,256,1]{2,1,0:T(8,128)S(1)} %copy-done.4, bf16[16,256,512]{2,1,0:T(8,128)(2,1)S(1)} %copy-done.5), custom_call_target="tpu_custom_call" | custom-call | tf_op jit(solution)/shard_map/grid/pallas_call | solution.py:396
  325.5 0.0 copy-start.3
  325.5 3.4 copy-done.3
  328.9 228.1 %adjoint.1 = bf16[4,16,128,512]{3,2,1,0:T(8,128)(2,1)} custom-call(s32[16]{0:T(128)} %dynamic_slice.3.waves_ref, bf16[4,16,16,16,256]{4,3,2,1,0:T(8,128)(2,1)} %copy-done.3, bf16[16,256,256]{2,1,0:T(8,128)(2,1)} %all-gather.2.cloned.1.call-done.l_ref, bf16[4,512,128]{2,1,0:T(8,128)(2,1)} %bitcast.20), custom_call_target="tpu_custom_call" | custom-call | tf_op jit(solution)/shard_map/adjoint/pallas_call | solution.py:415
  557.1 0.0 copy-start.1
  557.1 16.4 %copy.23 = bf16[2,2,16,128,512]{4,1,3,2,0:T(2,128)(2,1)} copy(bf16[2,2,16,128,512]{4,3,2,1,0:T(8,128)(2,1)} %bitcast.16) | data formatting | bytes 16777216 | tf_op jit(solution)/shard_map/reshape | solution.py:431
  573.5 0.0 copy-done.1
Async XLA Ops:
  7.2 12.7 %copy-start = (f32[8,256]{1,0:T(8,128)S(1)}, f32[8,256]{1,0:T(8,128)}, u32[]{:S(2)}) copy-start(f32[8,256]{1,0:T(8,128)} %param.14) | copy-start | bytes 24580
  7.2 36.2 %all-gather.2.cloned.1.call-start = ((), (), s32[]{:S(2)}) async-start(), calls=%async_computation | async-start | bytes 3145728 | tf_op jit(solution)/shard_map/all_gather | solution.py:368
  9.9 8.8 %copy-start.7 = (bf16[4,4,128,128]{3,2,1,0:T(8,128)(2,1)S(1)}, bf16[4,4,128,128]{3,2,1,0:T(8,128)(2,1)}, u32[]{:S(2)}) copy-start(bf16[4,4,128,128]{3,2,1,0:T(8,128)(2,1)} %param.11) | copy-start | bytes 1572868
  10.0 9.9 %copy-start.8 = (s32[16]{0:T(128)S(1)}, s32[16]{0:T(128)}, u32[]{:S(2)}) copy-start(s32[16]{0:T(128)} %param.13) | copy-start | bytes 196
  47.3 226.1 %copy-start.6 = (s32[16]{0:T(128)S(1)}, s32[16]{0:T(128)}, u32[]{:S(2)}) copy-start(s32[16]{0:T(128)} %points_ref.1) | copy-start | bytes 196
  273.5 3.4 copy-start.2
  276.8 1.6 copy-start.4
  278.4 2.2 copy-start.5
  325.5 3.4 copy-start.3
  557.1 16.5 %copy-start.1 = (f32[8,256]{1,0:T(8,128)S(1)}, f32[8,256]{1,0:T(8,128)}, u32[]{:S(2)}) copy-start(f32[8,256]{1,0:T(8,128)} %param.14) | copy-start | bytes 24580
Sparse Core Ops, SparseCore 0:
  9.5 33.8 all-gather.1

commit v2 on v1

--- a/solution.py
+++ b/solution.py
@@ -142,10 +142,10 @@
     return jnp.dot(stacked, matrix, preferred_element_type=jnp.float32).astype(jnp.bfloat16)
 
 
-def forward_kernel(n_wave, n_lev, waves, waves_ref, x_ref, lt_ref, v_ref, out_ref,
-                   spec, away, coef, wsend, x_send, x_recv, w_send, w_recv, own_sem):
+def forward_kernel(n_wave, n_lev, waves, waves_ref, x_ref, l_ref, v_ref, out_ref, full_ref,
+                   full, l_send, l_recv, full_sem, spec, away, coef, wsend, x_send, x_recv, w_send, w_recv, own_sem):
     chunks, slots, rows, _ = x_ref.shape
-    lats = lt_ref.shape[1] // n_wave
+    lats = l_ref.shape[2] // n_wave
     per = v_ref.shape[0] // n_lev
     me_w, me_l = enter(n_wave, n_lev)
     row0 = me_l * rows
@@ -166,6 +166,18 @@
 
     def own_copy(q):
         return pltpu.make_async_copy(wsend.at[q, me_w], out_ref.at[q, me_w], own_sem.at[q])
+
+    def table_copy(d):
+        peer = lax.rem(me_l + d, n_lev)
+        return pltpu.make_async_remote_copy(
+            src_ref=l_ref, dst_ref=full.at[me_l],
+            send_sem=l_send.at[d - 1], recv_sem=l_recv.at[d - 1],
+            device_id=(me_w, peer), device_id_type=MESH)
+
+    for d in range(1, n_lev):
+        table_copy(d).start()
+    full[me_l] = l_ref[...]
+    keep = pltpu.make_async_copy(full, full_ref, full_sem)
 
     for q in range(chunks):
         def vertical_slot(s, carry):
@@ -186,13 +198,17 @@
         for d in range(1, n_lev):
             lev_copy(q, d).start()
 
+    for d in range(1, n_lev):
+        table_copy(d).wait()
+    keep.start()
     for q in range(chunks):
         for d in range(1, n_lev):
             lev_copy(q, d).wait_recv()
 
         def legendre_slot(s, carry):
             field = jnp.concatenate([spec[q, l, s] for l in range(n_lev)], axis=0)
-            coef[s] = jnp.dot(lt_ref[s], field, preferred_element_type=jnp.float32)
+            table = jnp.concatenate([full[l, s] for l in range(n_lev)], axis=0)
+            coef[s] = lax.dot_general(table, field, (((0,), (0,)), ((), ())), preferred_element_type=jnp.float32)
             return carry
 
         lax.fori_loop(0, slots, legendre_slot, 0)
@@ -220,6 +236,7 @@
         own_copy(q).wait()
         for d in range(1, n_lev):
             lev_copy(q, d).wait_send()
+    keep.wait()
 
 
 def adjoint_kernel(n_wave, n_lev, waves, waves_ref, a_ref, l_ref, v_ref, out_ref,
@@ -270,7 +287,7 @@
             field = fine[:, s, :].astype(jnp.bfloat16)
             for d in range(n_lev):
                 half = lax.rem(me_l + d, n_lev)
-                table = l_ref[s, pl.ds(pl.multiple_of(half * rows, rows), rows), :]
+                table = l_ref[half, s]
                 y = jnp.dot(table, field, preferred_element_type=jnp.float32).astype(jnp.bfloat16)
                 if d == 0:
                     back[q, me_l, s] = y
@@ -365,19 +382,23 @@
     chunks = 2 * members
     bf16, f32 = jnp.bfloat16, jnp.float32
     own_waves = lax.dynamic_slice_in_dim(wave_of_slot, lax.axis_index("wave") * slots, slots)
-    table = lax.all_gather(legendre, "lev", axis=1, tiled=True)
     x = control.transpose(0, 3, 1, 2, 4).reshape(chunks, slots, rows, columns)
     stack_f = vertical.transpose(1, 0, 3, 2).reshape(variables, COV_BANDS * LEVELS, LEVELS)
     stack_g = vertical.transpose(1, 0, 2, 3).reshape(variables, COV_BANDS * LEVELS, LEVELS)
     vmem = pl.BlockSpec(memory_space=pltpu.VMEM)
     smem = pl.BlockSpec(memory_space=pltpu.SMEM)
     dma = pltpu.SemaphoreType.DMA
-    by_lat = pl.pallas_call(
+    by_lat, table = pl.pallas_call(
         functools.partial(forward_kernel, n_wave, n_lev, waves),
-        out_shape=jax.ShapeDtypeStruct((chunks, n_wave, lats, slots, cols), bf16),
+        out_shape=[
+            jax.ShapeDtypeStruct((chunks, n_wave, lats, slots, cols), bf16),
+            jax.ShapeDtypeStruct((n_lev, *legendre.shape), bf16),
+        ],
         in_specs=[smem, vmem, vmem, vmem],
-        out_specs=pl.BlockSpec(memory_space=pl.ANY),
+        out_specs=[pl.BlockSpec(memory_space=pl.ANY)] * 2,
         scratch_shapes=[
+            pltpu.VMEM((n_lev, *legendre.shape), bf16),
+            dma((n_lev - 1,)), dma((n_lev - 1,)), dma,
             pltpu.VMEM((chunks, n_lev, slots, rows, cols), bf16),
             pltpu.VMEM((chunks, n_lev - 1, slots, rows, cols), bf16),
             pltpu.VMEM((slots, n_wave * lats, cols), f32),
@@ -387,7 +408,7 @@
         ],
         compiler_params=pltpu.CompilerParams(collective_id=0, has_side_effects=True, vmem_limit_bytes=VMEM_BYTES),
         name="forward",
-    )(own_waves, x, table.transpose(0, 2, 1), stack_f)
+    )(own_waves, x, legendre, stack_f)
     chooser = (
         lat_band[:, None] == jnp.arange(grid_scale.shape[0], dtype=jnp.int32)[None, :]
     ).astype(f32)

time: 581 us -> 556 us (0.957)
  waiting for transfers between devices: 21.1 us -> 0 us
  Pallas kernels: 499 us -> 517 us
  between operations: 14.1 us -> 0.74 us
  local copies, waits for them, and re-layouts: 45.1 us -> 38.1 us
    all_gather x1 -> x0, waiting for transfers between devices: 20.4 us -> none  [shards_kernels(): table = lax.all_gather(legendre, 'lev', axis=1, tiled=True)]
    pallas_call x1, Pallas kernels: 226 us -> 245 us  [shards_kernels(): pl.pallas_call(functools.partial(forward_kernel, n_wave, n_lev, waves), o...]
  transfers between devices with their start and end apart: 1 -> 0, of which waited for: 1 -> 0; matrix products, arithmetic and copies ran while one was open for 3% -> 0% of each run, Pallas kernels for 0% -> 0%
where the time goes in v2:
time: 556 us
  Pallas kernels  517 us (93%)
  local copies, waits for them, and re-layouts  38.1 us (7%)
    pallas_call x1, Pallas kernels, shards_kernels(): pl.pallas_call(functools.partial(forward_kernel, n_wave, n_lev, waves), o...  245 us
    pallas_call x1, Pallas kernels, shards_kernels(): pl.pallas_call(functools.partial(adjoint_kernel, n_wave, n_lev, waves), o...  227 us
    pallas_call x1, Pallas kernels, shards_kernels(): pl.pallas_call(grid_kernel, grid=(lats,), out_shape=[jax.ShapeDtypeStruct...  44.9 us
    reshape x1, local copies, waits for them, and re-layouts, shards_kernels(): gradient.reshape(members, 2, slots, rows, columns).transpose(0, 2, 3, 1, 4)  16.4 us

profile of v2, /device:TPU:29, one launch (start us, length us, event | category | flops | bytes accessed | tf_op | source)
XLA Modules:
  0.0 555.8 jit_solution(13079671333902197970)
XLA Ops:
  0.6 0.0 copy-start
  0.7 1.3 dynamic_slice.3.waves_ref
  1.9 0.0 copy-start.6
  1.9 8.8 %copy.14 = bf16[2,2,16,128,512]{4,3,2,1,0:T(8,128)(2,1)} copy(bf16[2,2,16,128,512]{4,1,3,2,0:T(2,128)(2,1)} %bitcast.16) | data formatting | bytes 16777216 | tf_op jit(solution)/shard_map/transpose | solution.py:385
  10.7 0.0 copy-start.8
  10.7 0.0 copy-start.7
  10.7 0.0 copy-start.5
  10.7 0.0 copy-done.6
  10.7 1.0 copy.15
  11.7 244.6 %forward.1 = (bf16[4,16,16,16,256]{4,3,2,1,0:T(8,128)(2,1)}, bf16[2,16,128,256]{3,2,1,0:T(8,128)(2,1)}) custom-call(s32[16]{0:T(128)} %dynamic_slice.3.waves_ref, bf16[4,16,128,512]{3,2,1,0:T(8,128)(2,1)} %bitcast.15, bf16[16,128,256]{2,1,0:T(8,128)(2,1)} %l_ref.1, bf16[4,512,128]{2,1,0:T(8,128)(2,1)} %bitcast.18), custom_call_target="tpu_custom_call" | custom-call | tf_op jit(solution)/shard_map/forward/pallas_call | solution.py:391
  256.3 0.0 copy-done
  256.3 0.0 copy-done.8
  256.3 0.2 convolution_bitcast_fusion
  256.5 0.6 copy.17.scale_ref
  257.2 0.0 copy-done.7
  257.2 0.1 copy.16.waves_ref
  257.3 0.0 copy-done.5
  257.4 0.0 copy-start.2
  257.4 3.4 copy-done.2
  260.7 0.0 copy-start.4
  260.7 2.2 copy-done.4
  262.9 44.9 %grid.1 = (bf16[2,16,256,512]{3,2,1,0:T(8,128)(2,1)}, bf16[4,16,16,16,256]{4,3,2,1,0:T(8,128)(2,1)S(1)}) custom-call(f32[256,1]{1,0:T(8,128)S(1)} %copy.16.waves_ref, s32[16]{0:T(128)S(1)} %copy-done.5, bf16[4,16,16,16,256]{4,3,2,1,0:T(8,128)(2,1)S(1)} %copy-done.2, f32[16,256,1]{2,1,0:T(8,128)S(1)} %copy.17.scale_ref, bf16[16,256,512]{2,1,0:T(8,128)(2,1)S(1)} %copy-done.4), custom_call_target="tpu_custom_call" | custom-call | tf_op jit(solution)/shard_map/grid/pallas_call | solution.py:417
  307.8 0.0 copy-start.3
  307.8 3.4 copy-done.3
  311.2 0.8 copy.18
  312.1 227.3 %adjoint.1 = bf16[4,16,128,512]{3,2,1,0:T(8,128)(2,1)} custom-call(s32[16]{0:T(128)} %dynamic_slice.3.waves_ref, bf16[4,16,16,16,256]{4,3,2,1,0:T(8,128)(2,1)} %copy-done.3, bf16[2,16,128,256]{3,2,1,0:T(8,128)(2,1)} %get-tuple-element.9.l_ref, bf16[4,512,128]{2,1,0:T(8,128)(2,1)} %bitcast.19), custom_call_target="tpu_custom_call" | custom-call | tf_op jit(solution)/shard_map/adjoint/pallas_call | solution.py:436
  539.3 0.0 copy-start.1
  539.4 16.4 %copy.21 = bf16[2,2,16,128,512]{4,1,3,2,0:T(2,128)(2,1)} copy(bf16[2,2,16,128,512]{4,3,2,1,0:T(8,128)(2,1)} %bitcast.14) | data formatting | bytes 16777216 | tf_op jit(solution)/shard_map/reshape | solution.py:452
  555.8 0.0 copy-done.1
  (1 shorter events, 0.0 us)
Async XLA Ops:
  0.6 255.7 %copy-start = (f32[8,256]{1,0:T(8,128)S(1)}, f32[8,256]{1,0:T(8,128)}, u32[]{:S(2)}) copy-start(f32[8,256]{1,0:T(8,128)} %param.14) | copy-start | bytes 24580
  1.9 8.8 %copy-start.6 = (bf16[4,4,128,128]{3,2,1,0:T(8,128)(2,1)S(1)}, bf16[4,4,128,128]{3,2,1,0:T(8,128)(2,1)}, u32[]{:S(2)}) copy-start(bf16[4,4,128,128]{3,2,1,0:T(8,128)(2,1)} %param.11) | copy-start | bytes 1572868
  10.7 245.6 %copy-start.8 = (s32[16]{0:T(128)S(1)}, s32[16]{0:T(128)}, u32[]{:S(2)}) copy-start(s32[16]{0:T(128)} %param.13) | copy-start | bytes 196
  10.7 246.5 %copy-start.7 = (s32[256]{0:T(256)S(1)}, s32[256]{0:T(256)}, u32[]{:S(2)}) copy-start(s32[256]{0:T(256)} %param.9) | copy-start | bytes 3076
  10.7 246.6 %copy-start.5 = (s32[16]{0:T(128)S(1)}, s32[16]{0:T(128)}, u32[]{:S(2)}) copy-start(s32[16]{0:T(128)} %points_ref.1) | copy-start | bytes 196
  257.4 3.4 copy-start.2
  260.7 2.2 copy-start.4
  307.8 3.4 copy-start.3
  539.3 16.5 %copy-start.1 = (f32[8,256]{1,0:T(8,128)S(1)}, f32[8,256]{1,0:T(8,128)}, u32[]{:S(2)}) copy-start(f32[8,256]{1,0:T(8,128)} %param.14) | copy-start | bytes 24580
